TPU v7x, 32 devices: a whole 2x2x4 slice. The times are simulated.
32 devices in a mesh: section: 8 (over y, x, core), dp: 4 (over z).
Axes of the slice: x: 2, y: 2, z: 4, core: 2. Of those that a mesh axis runs over, the one named last changes fastest.
Arguments:
- out_pair: float32 [512, 2048], P('dp'), may hold values from -6 to 6
- out_grad: bfloat16 [512, 2048], P('dp'), may hold values from -6 to 6
- f_weight: bfloat16 [8, 1024, 1024], P('section', 'dp'), may hold values from -0.09375 to 0.09375
- g_weight: bfloat16 [8, 1024, 1024], P('section', 'dp'), may hold values from -0.09375 to 0.09375
- gains: float32 [8, 2, 1024], P('section'), may hold values from 0.1 to 1.9
Outputs:
- in_pair: float32 [8, 512, 2048], P('section', 'dp')
- in_grad: bfloat16 [8, 512, 2048], P('section', 'dp')
- f_grad: float32 [8, 1024, 1024], P('section', 'dp')
- g_grad: float32 [8, 1024, 1024], P('section', 'dp')
- gains_grad: float32 [8, 2, 1024], P('section')
All inputs are finite; a program needn't handle non-finite values.
Results may differ from a plain program's by a relative error of at most 0.04.
Values may be sent and summed in bfloat16 or wider, within the bound.
A program may use at most 64 MiB of HBM per device.

v0:
```python
import functools

import jax
import jax.numpy as jnp
from jax import lax
from jax.experimental import pallas as pl
from jax.experimental.pallas import tpu as pltpu
from jax.sharding import PartitionSpec as P

offset = 0.25
MESH = pl.DeviceIdType.MESH
f32, bf16 = jnp.float32, jnp.bfloat16


def silu_parts(pre_values):
    sigmoid_value = jax.nn.sigmoid(pre_values)
    return (pre_values * sigmoid_value, sigmoid_value * (1.0 + pre_values * (1.0 - sigmoid_value)))


def inverse_scale(values):
    return lax.rsqrt(jnp.mean(values * values, axis=-1, keepdims=True) + offset)


def kernel(
    n, sections, blocks,
    pair_ref, grad_ref, fw_ref, gw_ref, gains_ref,
    in_pair_ref, in_grad_ref, f_out, g_out, gain_out,
    wf, wg, wft, wgt, aside, late, rx, tx, held, slopes, norms_own, norms, deltas, gain_parts,
    l_sem, lh_send, lh_recv, lo_send, lo_recv, own_sem, i_send, i_recv, h_send, h_recv, o_send, o_recv, w_send, w_recv, p_send, p_recv, n_send, n_recv, d_send, d_recv, c_send, c_recv,
):
    s, d = lax.axis_index("section"), lax.axis_index("dp")
    is_last = s == sections - 1
    has_below = s > 0
    not_last = jnp.logical_not(is_last)
    tokens = pair_ref.shape[0]
    h = pair_ref.shape[1] // 2
    part = fw_ref.shape[0]
    rows_per = tokens // blocks

    def peer(k):
        return lax.rem(d + k, n)

    barrier = pltpu.get_barrier_semaphore()
    for k in range(1, n):
        pl.semaphore_signal(barrier, inc=1, device_id=(s, peer(k)), device_id_type=MESH)

    @pl.when(has_below)
    def _():
        pl.semaphore_signal(barrier, inc=1, device_id=(s - 1, d), device_id_type=MESH)

    @pl.when(not_last)
    def _():
        pl.semaphore_signal(barrier, inc=1, device_id=(s + 1, d), device_id_type=MESH)

    half = sections // 2
    partner = lax.rem(s + half, sections)
    high, low = s >= half, s < half
    pl.semaphore_signal(barrier, inc=1, device_id=(partner, d), device_id_type=MESH)
    neighbours = n + has_below.astype(jnp.int32) + not_last.astype(jnp.int32)
    pl.semaphore_wait(barrier, neighbours)

    fulls, owns, turned = (wg, wf), (gw_ref, fw_ref), (wgt, wft)
    keep = h - aside.shape[3]
    variants = ((low, pl.ds(0, h)), (high, pl.ds(0, keep)))
    rest = pl.ds(keep, h - keep)

    def shard(a, owner, cols):
        return fulls[a].at[pl.ds(pl.multiple_of(owner * part, part), part), cols]

    def owner_of(way, k):
        return d - k if way == 0 else d + k

    def ahead(way):
        return d + 1 if way == 0 else d - 1

    def hop(a, way, k, cols):
        owner = owner_of(way, k)
        src = owns[a].at[:, cols] if k == 0 else shard(a, owner, cols)
        return pltpu.make_async_remote_copy(
            src_ref=src, dst_ref=shard(a, owner, cols),
            send_sem=w_send.at[a, way, k], recv_sem=w_recv.at[a, way, k],
            device_id=(s, ahead(way)), device_id_type=MESH,
        )

    def aside_in(a):
        return pltpu.make_async_remote_copy(
            src_ref=owns[a].at[:, rest], dst_ref=aside.at[a, d],
            send_sem=i_send.at[a], recv_sem=i_recv.at[a],
            device_id=(partner, d), device_id_type=MESH,
        )

    def aside_hop(a, way, k):
        owner = owner_of(way, k)
        return pltpu.make_async_remote_copy(
            src_ref=aside.at[a, owner], dst_ref=aside.at[a, owner],
            send_sem=h_send.at[a, way, k], recv_sem=h_recv.at[a, way, k],
            device_id=(s, ahead(way)), device_id_type=MESH,
        )

    def aside_out(a, way, k):
        owner = owner_of(way, k)
        return pltpu.make_async_remote_copy(
            src_ref=aside.at[a, owner], dst_ref=shard(a, owner, rest),
            send_sem=o_send.at[a, way, k], recv_sem=o_recv.at[a, way, k],
            device_id=(partner, d), device_id_type=MESH,
        )

    def wait_bytes(ref, sem):
        pltpu.make_async_copy(ref, ref, sem).wait()

    def reach(way, k):
        if way == 0:
            return jnp.logical_and(d - k >= 0, d < n - 1)
        return jnp.logical_and(d + k < n, d > 0)

    def arrives(way, k):
        return d - k >= 0 if way == 0 else d + k < n

    both = jnp.logical_and

    @pl.when(high)
    def _():
        for a in range(2):
            aside_in(a).start()

    @pl.when(low)
    def _():
        for a in range(2):
            wait_bytes(aside.at[a, d], i_recv.at[a])
            for way in range(2):
                @pl.when(reach(way, 0))
                def _():
                    aside_hop(a, way, 0).start()

    for a in range(2):
        for way in range(2):
            for side, cols in variants:
                @pl.when(both(side, reach(way, 0)))
                def _():
                    hop(a, way, 0, cols).start()
    early = part % 128 == 0

    def turn(a, owner):
        span = pl.ds(pl.multiple_of(owner * part, part), part)
        turned[a][:, span] = fulls[a][span, :].T

    own_copies = [
        pltpu.make_async_copy(owns[a], shard(a, d, pl.ds(0, h)), own_sem.at[a]) for a in range(2)
    ]
    for copy in own_copies:
        copy.start()
    for a, copy in enumerate(own_copies):
        copy.wait()
        if early:
            turn(a, d)
    for k in range(1, n):
        for a in range(2):
            for way in range(2):
                @pl.when(both(low, arrives(way, k)))
                def _():
                    wait_bytes(aside.at[a, owner_of(way, k)], h_recv.at[a, way, k - 1])
                    if k < n - 1:
                        @pl.when(reach(way, k))
                        def _():
                            aside_hop(a, way, k).start()
                    aside_out(a, way, k).start()
        for a in range(2):
            for way in range(2):
                for side, cols in variants:
                    @pl.when(both(side, arrives(way, k)))
                    def _():
                        wait_bytes(shard(a, owner_of(way, k), cols), w_recv.at[a, way, k - 1])

                    if k < n - 1:
                        @pl.when(both(side, reach(way, k)))
                        def _():
                            hop(a, way, k, cols).start()
        for a in range(2):
            for way in range(2):
                @pl.when(both(high, arrives(way, k)))
                def _():
                    wait_bytes(shard(a, owner_of(way, k), rest), o_recv.at[a, way, k])

                if early:
                    @pl.when(arrives(way, k))
                    def _():
                        turn(a, owner_of(way, k))
    if not early:
        for a in range(2):
            turned[a][...] = fulls[a][...].T

    gain_out[...] = jnp.zeros_like(gain_out)

    def pair_copy(i, b):
        rows = pl.ds(pl.multiple_of(b * rows_per, rows_per), rows_per)
        return pltpu.make_async_remote_copy(
            src_ref=tx.at[i, rows], dst_ref=rx.at[i, rows],
            send_sem=p_send.at[i], recv_sem=p_recv.at[i, b],
            device_id=(s - 1, d), device_id_type=MESH,
        )

    def take(i, b, rows, source, column):
        @pl.when(is_last)
        def _():
            held[i] = source[rows, column].astype(f32)

        @pl.when(not_last)
        def _():
            rows_ = pl.ds(pl.multiple_of(b * rows_per, rows_per), rows_per)
            pltpu.make_async_remote_copy(
                src_ref=tx.at[i, rows_], dst_ref=rx.at[i, rows_],
                send_sem=p_send.at[i], recv_sem=p_recv.at[i, b],
                device_id=(s + 1, d), device_id_type=MESH,
            ).wait_recv()
            held[i] = rx[i, rows].astype(f32)

    def give(i, b, rows, values):
        tx[i, rows] = values.astype(bf16)

        @pl.when(has_below)
        def _():
            pair_copy(i, b).start()

    def share_norm(a, rows, normed):
        for e in range(n):
            norms_own[a, e, rows] = normed[:, e * part:(e + 1) * part]
        for k in range(1, n):
            e = peer(k)
            pltpu.make_async_remote_copy(
                src_ref=norms_own.at[a, e, rows], dst_ref=norms.at[a, d, rows],
                send_sem=n_send.at[a], recv_sem=n_recv.at[a],
                device_id=(s, e), device_id_type=MESH,
            ).start()

    split = h - late.shape[2]
    tail = pl.ds(split, h - split)
    delta_variants = (
        ((jnp.bool_(True), pl.ds(0, h)),), ((low, pl.ds(0, split)), (high, pl.ds(0, h))),
    )

    def late_in(rows):
        return pltpu.make_async_remote_copy(
            src_ref=deltas.at[1, d, rows, tail], dst_ref=late.at[d, rows],
            send_sem=l_sem.at[0], recv_sem=l_sem.at[1],
            device_id=(partner, d), device_id_type=MESH,
        )

    def late_hop(way, k):
        owner = owner_of(way, k)
        return pltpu.make_async_remote_copy(
            src_ref=late.at[owner], dst_ref=late.at[owner],
            send_sem=lh_send.at[way, k], recv_sem=lh_recv.at[way, k],
            device_id=(s, ahead(way)), device_id_type=MESH,
        )

    def late_out(way, k):
        owner = owner_of(way, k)
        return pltpu.make_async_remote_copy(
            src_ref=late.at[owner], dst_ref=deltas.at[1, owner, pl.ds(0, tokens), tail],
            send_sem=lo_send.at[way, k], recv_sem=lo_recv.at[way, k],
            device_id=(partner, d), device_id_type=MESH,
        )

    def delta_hop(a, way, k, rows, cols):
        owner = d - k if way == 0 else d + k
        return pltpu.make_async_remote_copy(
            src_ref=deltas.at[a, owner, rows, cols], dst_ref=deltas.at[a, owner, rows, cols],
            send_sem=d_send.at[a, way, k], recv_sem=d_recv.at[a, way, k],
            device_id=(s, d + 1 if way == 0 else d - 1), device_id_type=MESH,
        )

    def share_delta(a, rows, delta):
        deltas[a, d, rows] = delta
        for way in range(2):
            for side, cols in delta_variants[a]:
                @pl.when(both(side, reach(way, 0)))
                def _():
                    delta_hop(a, way, 0, rows, cols).start()
        if a == 1:
            @pl.when(low)
            def _():
                late_in(rows).start()

    first, second = pl.ds(0, h), pl.ds(h, h)

    def block(b, carry):
        rows = pl.ds(pl.multiple_of(b * rows_per, rows_per), rows_per)
        gain_f, gain_g = gains_ref[0:1, :], gains_ref[1:2, :]
        take(0, b, rows, pair_ref, first)
        y1 = held[0]
        r1 = inverse_scale(y1)
        norm_g = (y1 * r1 * gain_g).astype(bf16)
        pre_g = jnp.dot(norm_g, wg[...], preferred_element_type=f32)
        take(1, b, rows, pair_ref, second)
        act_g, slope_g = silu_parts(pre_g)
        x2 = held[1] - act_g
        in_pair_ref[rows, second] = x2
        give(1, b, rows, x2)
        slopes[0] = slope_g
        r2 = inverse_scale(x2)
        norm_f = (x2 * r2 * gain_f).astype(bf16)
        pre_f = jnp.dot(norm_f, wf[...], preferred_element_type=f32)
        act_f, slope_f = silu_parts(pre_f)
        x1 = held[0] - act_f
        in_pair_ref[rows, first] = x1
        give(0, b, rows, x1)
        slopes[1] = slope_f
        share_norm(0, rows, norm_f)
        share_norm(1, rows, norm_g)

        take(3, b, rows, grad_ref, second)
        take(2, b, rows, grad_ref, first)
        delta_g = (held[3] * slopes[0]).astype(bf16)
        back_g = jnp.dot(delta_g, wgt[...], preferred_element_type=f32)
        share_delta(1, rows, delta_g)
        y1 = held[0]
        weighted = gain_g * back_g
        gz = held[2] + r1 * weighted - y1 * (r1 * r1 * r1) * jnp.mean(
            weighted * y1, axis=-1, keepdims=True
        )
        in_grad_ref[rows, first] = gz.astype(bf16)
        give(2, b, rows, gz)
        gain_out[1:2, :] += jnp.sum(back_g * y1 * r1, axis=0, keepdims=True)
        delta_f = (gz * slopes[1]).astype(bf16)
        back_f = jnp.dot(delta_f, wft[...], preferred_element_type=f32)
        share_delta(0, rows, delta_f)
        x2 = in_pair_ref[rows, second]
        weighted = gain_f * back_f
        gx2 = held[3] + r2 * weighted - x2 * (r2 * r2 * r2) * jnp.mean(
            weighted * x2, axis=-1, keepdims=True
        )
        in_grad_ref[rows, second] = gx2.astype(bf16)
        give(3, b, rows, gx2)
        gain_out[0:1, :] += jnp.sum(back_f * x2 * r2, axis=0, keepdims=True)
        return carry

    lax.fori_loop(0, blocks, block, 0)

    gain_parts[d] = gain_out[...]
    for k in range(1, n):
        pltpu.make_async_remote_copy(
            src_ref=gain_parts.at[d], dst_ref=gain_parts.at[d],
            send_sem=c_send, recv_sem=c_recv,
            device_id=(s, peer(k)), device_id_type=MESH,
        ).start()

    for a in range(2):
        norms[a, d] = norms_own[a, d]
    others, whole = pl.ds(0, n - 1), pl.ds(0, tokens)
    for k in range(1, n):
        for a in (1, 0):
            for way in range(2):
                for side, cols in delta_variants[a]:
                    @pl.when(both(side, arrives(way, k)))
                    def _():
                        wait_bytes(
                            deltas.at[a, owner_of(way, k), whole, cols], d_recv.at[a, way, k - 1]
                        )

                    if k < n - 1:
                        @pl.when(both(side, reach(way, k)))
                        def _():
                            delta_hop(a, way, k, whole, cols).start()
    @pl.when(high)
    def _():
        wait_bytes(late.at[d], l_sem.at[1])
        for way in range(2):
            @pl.when(reach(way, 0))
            def _():
                late_hop(way, 0).start()

    for a, out in ((0, f_out), (1, g_out)):
        if a == 1:
            for k in range(1, n):
                for way in range(2):
                    @pl.when(both(low, arrives(way, k)))
                    def _():
                        wait_bytes(deltas.at[1, owner_of(way, k), whole, tail], lo_recv.at[way, k])
        wait_bytes(norms.at[a, others], n_recv.at[a])
        out[...] = lax.dot_general(
            norms[a].reshape(n * tokens, part), deltas[a].reshape(n * tokens, h),
            (((0,), (0,)), ((), ())), preferred_element_type=f32,
        )

    @pl.when(high)
    def _():
        for k in range(1, n):
            for way in range(2):
                @pl.when(arrives(way, k))
                def _():
                    wait_bytes(late.at[owner_of(way, k)], lh_recv.at[way, k - 1])
                    if k < n - 1:
                        @pl.when(reach(way, k))
                        def _():
                            late_hop(way, k).start()
                    late_out(way, k).start()
        for k in range(n):
            for way in range(2):
                if k < n - 1:
                    @pl.when(reach(way, k))
                    def _():
                        late_hop(way, k).wait_send()
                if k > 0:
                    @pl.when(arrives(way, k))
                    def _():
                        late_out(way, k).wait_send()

    @pl.when(low)
    def _():
        wait_bytes(late.at[d], l_sem.at[0])

    wait_bytes(gain_parts.at[others], c_recv)
    total = gain_parts[0]
    for e in range(1, n):
        total = total + gain_parts[e]
    gain_out[...] = total

    for a in range(2):
        wait_bytes(norms.at[a, others], n_send.at[a])
        for k in range(n - 1):
            for way in range(2):
                for side, cols in delta_variants[a]:
                    @pl.when(both(side, reach(way, k)))
                    def _():
                        wait_bytes(
                            deltas.at[a, owner_of(way, k), whole, cols], d_send.at[a, way, k]
                        )
    wait_bytes(gain_parts.at[others], c_send)

    @pl.when(has_below)
    def _():
        for i in range(4):
            wait_bytes(tx.at[i], p_send.at[i])

    @pl.when(high)
    def _():
        for a in range(2):
            aside_in(a).wait_send()

    for k in range(n):
        for a in range(2):
            for way in range(2):
                if k < n - 1:
                    for side, cols in variants:
                        @pl.when(both(side, reach(way, k)))
                        def _():
                            hop(a, way, k, cols).wait_send()

                    @pl.when(both(low, reach(way, k)))
                    def _():
                        aside_hop(a, way, k).wait_send()
                if k > 0:
                    @pl.when(both(low, arrives(way, k)))
                    def _():
                        aside_out(a, way, k).wait_send()


def shards(out_pair, out_grad, f_weight, g_weight, gains):
    n, sections = lax.axis_size("dp"), lax.axis_size("section")
    tokens, width = out_pair.shape
    h = width // 2
    part = f_weight.shape[1]
    blocks = 4
    vmem = pl.BlockSpec(memory_space=pltpu.VMEM)
    dma = pltpu.SemaphoreType.DMA
    outs = pl.pallas_call(
        functools.partial(kernel, n, sections, blocks),
        out_shape=(
            jax.ShapeDtypeStruct((tokens, width), f32),
            jax.ShapeDtypeStruct((tokens, width), bf16),
            jax.ShapeDtypeStruct((part, h), f32),
            jax.ShapeDtypeStruct((part, h), f32),
            jax.ShapeDtypeStruct((2, h), f32),
        ),
        in_specs=[vmem] * 5,
        out_specs=[vmem] * 5,
        scratch_shapes=[
            pltpu.VMEM((h, h), bf16),
            pltpu.VMEM((h, h), bf16),
            pltpu.VMEM((h, h), bf16),
            pltpu.VMEM((h, h), bf16),
            pltpu.VMEM((2, n, part, h // 8), bf16),
            pltpu.VMEM((n, tokens, h // 2), bf16),
            pltpu.VMEM((4, tokens, h), bf16),
            pltpu.VMEM((4, tokens, h), bf16),
            pltpu.VMEM((4, tokens // blocks, h), f32),
            pltpu.VMEM((2, tokens // blocks, h), f32),
            pltpu.VMEM((2, n, tokens, part), bf16),
            pltpu.VMEM((2, n, tokens, part), bf16),
            pltpu.VMEM((2, n, tokens, h), bf16),
            pltpu.VMEM((n, 2, h), f32),
            dma((2,)),
            dma((2, n)),
            dma((2, n)),
            dma((2, n)),
            dma((2, n)),
            dma((2,)),
            dma((2,)),
            dma((2,)),
            dma((2, 2, n)),
            dma((2, 2, n)),
            dma((2, 2, n)),
            dma((2, 2, n)),
            dma((2, 2, n)),
            dma((2, 2, n)),
            dma((4,)),
            dma((4, blocks)),
            dma((2,)),
            dma((2,)),
            dma((2, 2, n)),
            dma((2, 2, n)),
            dma,
            dma,
        ],
        compiler_params=pltpu.CompilerParams(
            collective_id=0, has_side_effects=True, vmem_limit_bytes=60 * 1024 * 1024
        ),
    )(out_pair, out_grad, f_weight[0], g_weight[0], gains[0])
    return tuple(out[None] for out in outs)


def solution(mesh):
    placed = (
        P("dp", None),
        P("dp", None),
        P("section", "dp", None),
        P("section", "dp", None),
        P("section", None, None),
    )
    return jax.shard_map(
        shards,
        mesh=mesh,
        in_specs=placed,
        out_specs=(
            P("section", "dp", None),
            P("section", "dp", None),
            P("section", "dp", None),
            P("section", "dp", None),
            P("section", None, None),
        ),
        check_vma=False,
    )
```

profile of v0, /device:TPU:0, one launch (start us, length us, event | category | flops | bytes accessed | tf_op | source)
XLA Modules:
  0.0 147.6 jit_solution(2579741044289205113)
XLA Ops:
  0.6 140.5 %shard_map.92 = (f32[128,2048]{1,0:T(8,128)}, bf16[128,2048]{1,0:T(8,128)(2,1)}, f32[256,1024]{1,0:T(8,128)}, f32[256,1024]{1,0:T(8,128)}, f32[2,1024]{1,0:T(2,128)}) custom-call(f32[128,2048]{1,0:T(8,128)} %pair_ref.1, bf16[128,2048]{1,0:T(8,128)(2,1)} %grad_ref.1, bf16[256,1024]{1,0:T(8,128)(2,1)} %bitcast.11, bf16[256,1024]{1,0:T(8,128)(2,1)} %bitcast.12, ...), custom_call_target="tpu_custom_call" | custom-call | tf_op jit(solution)/shard_map/pallas_call | solution.py:466
  141.2 0.0 copy-start.2
  141.2 0.0 copy-start.1
  141.2 2.4 %copy.15 = f32[1,128,2048]{2,1,0:T(8,128)} copy(f32[1,128,2048]{2,1,0:T(8,128)} %bitcast.10) | data formatting | bytes 2097152
  143.6 0.0 copy-done.2
  143.6 0.8 copy.16
  144.4 0.0 copy-done.1
  144.4 0.0 copy-start
  144.4 1.0 copy.17
  145.4 0.6 copy-done
  146.0 0.0 copy-start.3
  146.0 1.0 copy.18
  147.0 0.0 copy-done.3
  147.0 0.6 copy.19
Async XLA Ops:
  141.2 2.4 %copy-start.2 = (bf16[128,2048]{1,0:T(8,128)(2,1)S(1)}, bf16[128,2048]{1,0:T(8,128)(2,1)}, u32[]{:S(2)}) copy-start(bf16[128,2048]{1,0:T(8,128)(2,1)} %get-tuple-element.11) | copy-start | bytes 1572868
  141.2 3.2 %copy-start.1 = (f32[256,1024]{1,0:T(8,128)S(1)}, f32[256,1024]{1,0:T(8,128)}, u32[]{:S(2)}) copy-start(f32[256,1024]{1,0:T(8,128)} %get-tuple-element.12) | copy-start | bytes 3145732
  144.4 1.6 %copy-start = (f32[256,1024]{1,0:T(8,128)S(1)}, f32[256,1024]{1,0:T(8,128)}, u32[]{:S(2)}) copy-start(f32[256,1024]{1,0:T(8,128)} %get-tuple-element.13) | copy-start | bytes 3145732
  146.0 1.0 copy-start.3
where the time goes:
time: 148 us
  Pallas kernels  141 us (95%)
  local copies, waits for them, and re-layouts  6.39 us (4%)
    pallas_call x1, Pallas kernels, shards(): pl.pallas_call(functools.partial(kernel, n, sections, blocks), out_shape=...  141 us
    unnamed x13, local copies, waits for them, and re-layouts  6.39 us

commit v1 on v0

v1 whole, which is shorter than its diff:
```python
import functools

import jax
import jax.numpy as jnp
from jax import lax
from jax.experimental import pallas as pl
from jax.experimental.pallas import tpu as pltpu
from jax.sharding import PartitionSpec as P

offset = 0.25
MESH = pl.DeviceIdType.MESH
f32, bf16 = jnp.float32, jnp.bfloat16


def silu_parts(pre_values):
    sigmoid_value = jax.nn.sigmoid(pre_values)
    return (pre_values * sigmoid_value, sigmoid_value * (1.0 + pre_values * (1.0 - sigmoid_value)))


def inverse_scale(values):
    return lax.rsqrt(jnp.mean(values * values, axis=-1, keepdims=True) + offset)


def kernel(
    n, sections, blocks,
    pair_ref, grad_ref, fw_ref, gw_ref, gains_ref,
    in_pair_ref, in_grad_ref, f_out, g_out, gain_out,
    wf, wg, wft, wgt, relay, rx, tx, held, slopes, norms_own, norms, deltas, result_tx, result_rx, gain_acc, gain_parts,
    go_sem, w_send, w_recv, r_send, r_recv, feed_send,
    p_send, p_recv, m_send, m_recv, n_send, n_recv, d_send, d_recv, c_send, c_recv, e_send, e_recv,
):
    s, d = lax.axis_index("section"), lax.axis_index("dp")
    m = n // 2
    half = sections // 2
    tokens = pair_ref.shape[0]
    h = pair_ref.shape[1] // 2
    part = fw_ref.shape[0]
    rows_all = 2 * tokens
    rows_per = rows_all // blocks
    own_blocks = blocks // 2

    pair_index = lax.div(d, 2)
    parity = lax.rem(pair_index, 2)
    host, mate = 2 * pair_index + 1 - parity, 2 * pair_index + parity
    is_host, is_mate = d == host, d == mate
    hosts = [2 * j + 1 - j % 2 for j in range(m)]

    is_last = s == sections - 1
    has_below = s > 0
    not_last = jnp.logical_not(is_last)
    partner = lax.rem(s + half, sections)
    high, low = s >= half, s < half
    both = jnp.logical_and

    chained = half % 2 == 0
    odd = lax.rem(s, 2) == 1
    even = jnp.logical_not(odd)
    crossing = jnp.where(high, s - half + 1, s + half - 1)
    crosses = both(even, high) | both(odd, low)
    follows = jnp.logical_not(both(odd, high))
    leads = jnp.logical_not(both(even, low))
    follower = jnp.where(odd, s - 1, crossing)
    feeds = both(s == half, is_mate)
    is_fed = both(is_last, is_host)

    barrier = pltpu.get_barrier_semaphore()

    def greet(section, replica):
        pl.semaphore_signal(barrier, inc=1, device_id=(section, replica), device_id_type=MESH)

    for k in range(1, n):
        greet(s, lax.rem(d + k, n))
    for k in range(n):
        greet(partner, lax.rem(d + k, n))

    @pl.when(has_below)
    def _():
        greet(s - 1, d)

    @pl.when(not_last)
    def _():
        greet(s + 1, d)

    @pl.when(feeds)
    def _():
        greet(sections - 1, host)

    @pl.when(is_fed)
    def _():
        greet(half, mate)

    neighbours = 2 * n - 1 + has_below.astype(jnp.int32) + not_last.astype(jnp.int32)
    neighbours += feeds.astype(jnp.int32) + is_fed.astype(jnp.int32)
    if chained:
        @pl.when(crosses)
        def _():
            greet(crossing, d)

        neighbours += crosses.astype(jnp.int32)
    pl.semaphore_wait(barrier, neighbours)

    fulls, owns = (wf, wg), (fw_ref, gw_ref)
    order = (1, 0)
    pieces = 2
    first, second = pl.ds(0, h), pl.ds(h, h)

    def wait_bytes(ref, sem):
        pltpu.make_async_copy(ref, ref, sem).wait()

    def send(src, dst, send_sem, recv_sem, section, replica):
        pltpu.make_async_remote_copy(
            src_ref=src, dst_ref=dst, send_sem=send_sem, recv_sem=recv_sem,
            device_id=(section, replica), device_id_type=MESH,
        ).start()

    def shard(a, owner, lead=0, size=part):
        start = pl.multiple_of(owner * part, part) + lead
        return fulls[a].at[pl.ds(pl.multiple_of(start, size), size)]

    def block_rows(b):
        return pl.ds(pl.multiple_of(b * rows_per, rows_per), rows_per)

    @pl.when(feeds)
    def _():
        for i, (source, column) in enumerate(
            ((pair_ref, first), (pair_ref, second), (grad_ref, first), (grad_ref, second))
        ):
            tx[i, pl.ds(tokens, tokens)] = source[:, column].astype(bf16)
        for b in range(own_blocks, blocks):
            for i in (0, 1, 3, 2):
                rows = block_rows(b)
                send(
                    tx.at[i, rows], rx.at[i, rows], feed_send, p_recv.at[i, b],
                    sections - 1, host,
                )

    def weights_out():
        if chained:
            @pl.when(follows)
            def _():
                pl.semaphore_wait(go_sem, 1)

        @pl.when(is_host)
        def _():
            for a in order:
                for t in hosts:
                    @pl.when(d != t)
                    def _():
                        send(owns[a], shard(a, d), w_send.at[a], w_recv.at[a], s, t)
            for a in order:
                fulls[a][pl.ds(pl.multiple_of(d * part, part), part), :] = owns[a][...]
            if m > 1:
                for a in order:
                    wait_bytes(fulls[a].at[pl.ds(0, (m - 1) * part)], w_send.at[a])

        @pl.when(is_mate)
        def _():
            for a in order:
                if m > 1:
                    for c in range(pieces):
                        size = part // pieces
                        rows = pl.ds(c * size, size)
                        send(
                            owns[a].at[rows], relay.at[a, rows], w_send.at[a], r_recv.at[a, c],
                            partner, d,
                        )
                send(owns[a], shard(a, d), w_send.at[a], w_recv.at[a], s, host)
            for a in order:
                wait_bytes(fulls[a].at[pl.ds(0, (2 if m > 1 else 1) * part)], w_send.at[a])

        if chained:
            @pl.when(leads)
            def _():
                pl.semaphore_signal(go_sem, inc=1, device_id=(follower, d), device_id_type=MESH)

    def pass_on():
        if m > 1:
            for a in order:
                for c in range(pieces):
                    size = part // pieces
                    rows = pl.ds(c * size, size)
                    wait_bytes(relay.at[a, rows], r_recv.at[a, c])
                    for t in hosts:
                        @pl.when(host != t)
                        def _():
                            send(
                                relay.at[a, rows], shard(a, d, c * size, size), r_send,
                                w_recv.at[a], partner, t,
                            )

    @pl.when(both(is_mate, low))
    def _():
        pass_on()

    weights_out()

    @pl.when(both(is_mate, high))
    def _():
        pass_on()

    def take(i, b, rows, source, column):
        local = both(is_last, b < own_blocks)

        @pl.when(local)
        def _():
            held[i] = source[rows, column].astype(f32)

        @pl.when(jnp.logical_not(local))
        def _():
            wait_bytes(rx.at[i, rows], p_recv.at[i, b])
            held[i] = rx[i, rows].astype(f32)

    def give(i, b, rows, values):
        tx[i, rows] = values.astype(bf16)

        @pl.when(has_below)
        def _():
            send(tx.at[i, rows], rx.at[i, rows], p_send, p_recv.at[i, b], s - 1, d)

        @pl.when(b >= own_blocks)
        def _():
            send(tx.at[i, rows], rx.at[i, rows], m_send, m_recv.at[i, b], s, mate)

    def share_norm(a, rows):
        for j, t in enumerate(hosts):
            @pl.when(d != t)
            def _():
                send(
                    norms_own.at[a, pl.ds(2 * j, 2), rows],
                    norms.at[a, pl.ds(0, 2), pair_index, rows],
                    n_send.at[a], n_recv.at[a], s, t,
                )

    def share_delta(a, rows):
        for t in hosts:
            @pl.when(d != t)
            def _():
                send(
                    deltas.at[a, pair_index, rows], deltas.at[a, pair_index, rows],
                    d_send.at[a], d_recv.at[a], s, t,
                )

    def block(b, carry):
        rows = block_rows(b)
        is_own = b < own_blocks
        gain_f, gain_g = gains_ref[0:1, :], gains_ref[1:2, :]
        take(0, b, rows, pair_ref, first)
        y1 = held[0]
        r1 = inverse_scale(y1)
        norm_g = (y1 * r1 * gain_g).astype(bf16)
        pre_g = jnp.dot(norm_g, wg[...], preferred_element_type=f32)
        take(1, b, rows, pair_ref, second)
        act_g, slope_g = silu_parts(pre_g)
        x2 = held[1] - act_g
        give(1, b, rows, x2)
        held[1] = x2
        slopes[0] = slope_g

        @pl.when(is_own)
        def _():
            in_pair_ref[rows, second] = x2

        r2 = inverse_scale(x2)
        norm_f = (x2 * r2 * gain_f).astype(bf16)

        @pl.when(b == 0)
        def _():
            wait_bytes(wf.at[pl.ds(0, (n - 1) * part)], w_recv.at[0])

        pre_f = jnp.dot(norm_f, wf[...], preferred_element_type=f32)
        act_f, slope_f = silu_parts(pre_f)
        x1 = held[0] - act_f
        give(0, b, rows, x1)
        slopes[1] = slope_f

        @pl.when(is_own)
        def _():
            in_pair_ref[rows, first] = x1

        for e in range(n):
            norms_own[0, e, rows] = norm_f[:, e * part:(e + 1) * part]
            norms_own[1, e, rows] = norm_g[:, e * part:(e + 1) * part]

        @pl.when(low)
        def _():
            share_norm(1, rows)
            share_norm(0, rows)

        @pl.when(b == 0)
        def _():
            wgt[...] = wg[...].T
            wft[...] = wf[...].T

        take(3, b, rows, grad_ref, second)
        take(2, b, rows, grad_ref, first)
        delta_g = (held[3] * slopes[0]).astype(bf16)
        back_g = jnp.dot(delta_g, wgt[...], preferred_element_type=f32)
        deltas[1, pair_index, rows] = delta_g

        @pl.when(low)
        def _():
            share_delta(1, rows)

        y1 = held[0]
        weighted = gain_g * back_g
        gz = held[2] + r1 * weighted - y1 * (r1 * r1 * r1) * jnp.mean(
            weighted * y1, axis=-1, keepdims=True
        )
        give(2, b, rows, gz)

        @pl.when(is_own)
        def _():
            in_grad_ref[rows, first] = gz.astype(bf16)

        gain_acc[1:2, :] += jnp.sum(back_g * y1 * r1, axis=0, keepdims=True)
        delta_f = (gz * slopes[1]).astype(bf16)
        back_f = jnp.dot(delta_f, wft[...], preferred_element_type=f32)
        deltas[0, pair_index, rows] = delta_f

        @pl.when(low)
        def _():
            share_delta(0, rows)

        x2 = held[1]
        weighted = gain_f * back_f
        gx2 = held[3] + r2 * weighted - x2 * (r2 * r2 * r2) * jnp.mean(
            weighted * x2, axis=-1, keepdims=True
        )
        give(3, b, rows, gx2)

        @pl.when(is_own)
        def _():
            in_grad_ref[rows, second] = gx2.astype(bf16)

        gain_acc[0:1, :] += jnp.sum(back_f * x2 * r2, axis=0, keepdims=True)
        return carry

    whole = pl.ds(0, rows_all)
    outs = (f_out, g_out)

    def product(a, which):
        return lax.dot_general(
            norms[a, which].reshape(m * rows_all, part), deltas[a].reshape(m * rows_all, h),
            (((0,), (0,)), ((), ())), preferred_element_type=f32,
        )

    @pl.when(is_host)
    def _():
        gain_acc[...] = jnp.zeros_like(gain_acc)
        wait_bytes(wg.at[pl.ds(0, (n - 1) * part)], w_recv.at[1])
        lax.fori_loop(0, blocks, block, 0)

        @pl.when(high)
        def _():
            for a in order:
                share_norm(a, whole)
                share_delta(a, whole)

        gain_parts[pair_index] = gain_acc[...]
        for k in range(1, n):
            send(
                gain_parts.at[pair_index], gain_parts.at[pair_index], c_send, c_recv,
                s, lax.rem(d + k, n),
            )
        for a in range(2):
            for w in range(2):
                norms[a, w, pair_index] = norms_own[a, 2 * pair_index + w]
        for a in order:
            if m > 1:
                wait_bytes(norms.at[a, pl.ds(0, 2), pl.ds(0, m - 1)], n_recv.at[a])
                wait_bytes(deltas.at[a, pl.ds(0, m - 1)], d_recv.at[a])
            result_tx[a] = product(a, parity).astype(bf16)
            send(result_tx.at[a], result_rx.at[a], e_send.at[a], e_recv.at[a], s, mate)
        for a in order:
            outs[a][...] = product(a, 1 - parity)

    @pl.when(is_mate)
    def _():
        def collect(b, carry):
            rows = block_rows(b + own_blocks)
            local = block_rows(b)
            for i, target, column in (
                (1, in_pair_ref, second), (0, in_pair_ref, first),
                (2, in_grad_ref, first), (3, in_grad_ref, second),
            ):
                wait_bytes(rx.at[i, rows], m_recv.at[i, b + own_blocks])
                target[local, column] = rx[i, rows].astype(target.dtype)
            return carry

        lax.fori_loop(0, own_blocks, collect, 0)
        for a in order:
            wait_bytes(result_rx.at[a], e_recv.at[a])
            outs[a][...] = result_rx[a].astype(f32)

    @pl.when(is_mate)
    def _():
        wait_bytes(gain_parts.at[pl.ds(0, m)], c_recv)

    if m > 1:
        @pl.when(is_host)
        def _():
            wait_bytes(gain_parts.at[pl.ds(0, m - 1)], c_recv)

    total = gain_parts[0]
    for j in range(1, m):
        total = total + gain_parts[j]
    gain_out[...] = total

    @pl.when(is_host)
    def _():
        wait_bytes(gain_parts.at[pl.ds(0, n - 1)], c_send)
        for a in range(2):
            wait_bytes(result_tx.at[a], e_send.at[a])
            if m > 1:
                wait_bytes(norms.at[a, pl.ds(0, 2), pl.ds(0, m - 1)], n_send.at[a])
                wait_bytes(deltas.at[a, pl.ds(0, m - 1)], d_send.at[a])
        wait_bytes(tx.at[:, pl.ds(0, tokens)], m_send)

        @pl.when(has_below)
        def _():
            wait_bytes(tx, p_send)

    if m > 1:
        @pl.when(is_mate)
        def _():
            for k in range(m - 1):
                wait_bytes(relay, r_send)

    @pl.when(feeds)
    def _():
        wait_bytes(tx.at[:, pl.ds(0, tokens)], feed_send)


def shards(out_pair, out_grad, f_weight, g_weight, gains):
    n, sections = lax.axis_size("dp"), lax.axis_size("section")
    tokens, width = out_pair.shape
    h = width // 2
    part = f_weight.shape[1]
    blocks = 4
    m = n // 2
    rows_all = 2 * tokens
    vmem = pl.BlockSpec(memory_space=pltpu.VMEM)
    dma = pltpu.SemaphoreType.DMA
    outs = pl.pallas_call(
        functools.partial(kernel, n, sections, blocks),
        out_shape=(
            jax.ShapeDtypeStruct((tokens, width), f32),
            jax.ShapeDtypeStruct((tokens, width), bf16),
            jax.ShapeDtypeStruct((part, h), f32),
            jax.ShapeDtypeStruct((part, h), f32),
            jax.ShapeDtypeStruct((2, h), f32),
        ),
        in_specs=[vmem] * 5,
        out_specs=[vmem] * 5,
        scratch_shapes=[
            pltpu.VMEM((h, h), bf16),
            pltpu.VMEM((h, h), bf16),
            pltpu.VMEM((h, h), bf16),
            pltpu.VMEM((h, h), bf16),
            pltpu.VMEM((2, part, h), bf16),
            pltpu.VMEM((4, rows_all, h), bf16),
            pltpu.VMEM((4, rows_all, h), bf16),
            pltpu.VMEM((4, rows_all // blocks, h), f32),
            pltpu.VMEM((2, rows_all // blocks, h), f32),
            pltpu.VMEM((2, n, rows_all, part), bf16),
            pltpu.VMEM((2, 2, m, rows_all, part), bf16),
            pltpu.VMEM((2, m, rows_all, h), bf16),
            pltpu.VMEM((2, part, h), bf16),
            pltpu.VMEM((2, part, h), bf16),
            pltpu.VMEM((2, h), f32),
            pltpu.VMEM((n, 2, h), f32),
            pltpu.SemaphoreType.REGULAR,
            dma((2,)),
            dma((2,)),
            dma,
            dma((2, 2)),
            dma,
            dma,
            dma((4, blocks)),
            dma,
            dma((4, blocks)),
            dma((2,)),
            dma((2,)),
            dma((2,)),
            dma((2,)),
            dma,
            dma,
            dma((2,)),
            dma((2,)),
        ],
        compiler_params=pltpu.CompilerParams(
            collective_id=0, has_side_effects=True, vmem_limit_bytes=60 * 1024 * 1024
        ),
    )(out_pair, out_grad, f_weight[0], g_weight[0], gains[0])
    return tuple(out[None] for out in outs)


def solution(mesh):
    placed = (
        P("dp", None),
        P("dp", None),
        P("section", "dp", None),
        P("section", "dp", None),
        P("section", None, None),
    )
    return jax.shard_map(
        shards,
        mesh=mesh,
        in_specs=placed,
        out_specs=(
            P("section", "dp", None),
            P("section", "dp", None),
            P("section", "dp", None),
            P("section", "dp", None),
            P("section", None, None),
        ),
        check_vma=False,
    )
```

time: 148 us -> 149 us (level)
  no operation moved by 1% of the time
where the time goes in v1:
time: 149 us
  Pallas kernels  142 us (95%)
  local copies, waits for them, and re-layouts  6.39 us (4%)
    pallas_call x1, Pallas kernels, shards(): pl.pallas_call(functools.partial(kernel, n, sections, blocks), out_shape=...  142 us
    unnamed x13, local copies, waits for them, and re-layouts  6.39 us

profile of v1, /device:TPU:0, one launch (start us, length us, event | category | flops | bytes accessed | tf_op | source)
XLA Modules:
  0.0 149.1 jit_solution(11013452117148208293)
XLA Ops:
  0.6 142.0 %shard_map.92 = (f32[128,2048]{1,0:T(8,128)}, bf16[128,2048]{1,0:T(8,128)(2,1)}, f32[256,1024]{1,0:T(8,128)}, f32[256,1024]{1,0:T(8,128)}, f32[2,1024]{1,0:T(2,128)}) custom-call(f32[128,2048]{1,0:T(8,128)} %pair_ref.1, bf16[128,2048]{1,0:T(8,128)(2,1)} %grad_ref.1, bf16[256,1024]{1,0:T(8,128)(2,1)} %bitcast.11, bf16[256,1024]{1,0:T(8,128)(2,1)} %bitcast.12, ...), custom_call_target="tpu_custom_call" | custom-call | tf_op jit(solution)/shard_map/pallas_call | solution.py:444
  142.7 0.0 copy-start.2
  142.7 0.0 copy-start.1
  142.7 2.4 %copy.15 = f32[1,128,2048]{2,1,0:T(8,128)} copy(f32[1,128,2048]{2,1,0:T(8,128)} %bitcast.10) | data formatting | bytes 2097152
  145.1 0.0 copy-done.2
  145.1 0.8 copy.16
  145.9 0.0 copy-done.1
  145.9 0.0 copy-start
  145.9 1.0 copy.17
  146.9 0.6 copy-done
  147.5 0.0 copy-start.3
  147.5 1.0 copy.18
  148.5 0.0 copy-done.3
  148.5 0.6 copy.19
Async XLA Ops:
  142.7 2.4 %copy-start.2 = (bf16[128,2048]{1,0:T(8,128)(2,1)S(1)}, bf16[128,2048]{1,0:T(8,128)(2,1)}, u32[]{:S(2)}) copy-start(bf16[128,2048]{1,0:T(8,128)(2,1)} %get-tuple-element.11) | copy-start | bytes 1572868
  142.7 3.2 %copy-start.1 = (f32[256,1024]{1,0:T(8,128)S(1)}, f32[256,1024]{1,0:T(8,128)}, u32[]{:S(2)}) copy-start(f32[256,1024]{1,0:T(8,128)} %get-tuple-element.12) | copy-start | bytes 3145732
  145.9 1.6 %copy-start = (f32[256,1024]{1,0:T(8,128)S(1)}, f32[256,1024]{1,0:T(8,128)}, u32[]{:S(2)}) copy-start(f32[256,1024]{1,0:T(8,128)} %get-tuple-element.13) | copy-start | bytes 3145732
  147.5 1.0 copy-start.3

commit v2 on v1

--- a/solution.py
+++ b/solution.py
@@ -26,7 +26,7 @@
     pair_ref, grad_ref, fw_ref, gw_ref, gains_ref,
     in_pair_ref, in_grad_ref, f_out, g_out, gain_out,
     wf, wg, wft, wgt, relay, rx, tx, held, slopes, norms_own, norms, deltas, result_tx, result_rx, gain_acc, gain_parts,
-    go_sem, w_send, w_recv, r_send, r_recv, feed_send,
+    go_sem, clear_sem, w_send, w_recv, r_send, r_recv, feed_send,
     p_send, p_recv, m_send, m_recv, n_send, n_recv, d_send, d_recv, c_send, c_recv, e_send, e_recv,
 ):
     s, d = lax.axis_index("section"), lax.axis_index("dp")
@@ -55,12 +55,13 @@
     chained = half % 2 == 0
     odd = lax.rem(s, 2) == 1
     even = jnp.logical_not(odd)
-    crossing = jnp.where(high, s - half + 1, s + half - 1)
-    crosses = both(even, high) | both(odd, low)
     follows = jnp.logical_not(both(odd, high))
-    leads = jnp.logical_not(both(even, low))
-    follower = jnp.where(odd, s - 1, crossing)
-    feeds = both(s == half, is_mate)
+    splits = both(even, high)
+    halves = both(even, low)
+    holds = both(both(odd, low), s > 1)
+    early = both(splits, s < sections - 2)
+    feeder = max(sections - 3, 0)
+    feeds = both(s == feeder, is_mate)
     is_fed = both(is_last, is_host)
 
     barrier = pltpu.get_barrier_semaphore()
@@ -87,21 +88,35 @@
 
     @pl.when(is_fed)
     def _():
-        greet(half, mate)
+        greet(feeder, mate)
 
     neighbours = 2 * n - 1 + has_below.astype(jnp.int32) + not_last.astype(jnp.int32)
     neighbours += feeds.astype(jnp.int32) + is_fed.astype(jnp.int32)
     if chained:
-        @pl.when(crosses)
-        def _():
-            greet(crossing, d)
-
-        neighbours += crosses.astype(jnp.int32)
+        @pl.when(splits)
+        def _():
+            greet(s - half + 1, d)
+
+        @pl.when(both(odd, low))
+        def _():
+            greet(s + half - 1, d)
+
+        neighbours += (splits | both(odd, low)).astype(jnp.int32)
+
+        @pl.when(both(high, both(even, is_mate)))
+        def _():
+            greet(s + 1, host)
+
+        @pl.when(both(high, both(odd, is_host)))
+        def _():
+            greet(s - 1, mate)
+
+        neighbours += both(high, both(even, is_mate) | both(odd, is_host)).astype(jnp.int32)
     pl.semaphore_wait(barrier, neighbours)
 
     fulls, owns = (wf, wg), (fw_ref, gw_ref)
     order = (1, 0)
-    pieces = 2
+    pieces = 4
     first, second = pl.ds(0, h), pl.ds(h, h)
 
     def wait_bytes(ref, sem):
@@ -120,8 +135,11 @@
     def block_rows(b):
         return pl.ds(pl.multiple_of(b * rows_per, rows_per), rows_per)
 
-    @pl.when(feeds)
-    def _():
+    def place_of(b):
+        later = jnp.where(b <= own_blocks, b - 1 + own_blocks, b - own_blocks)
+        return jnp.where(b == 0, 0, later)
+
+    def feed():
         for i, (source, column) in enumerate(
             ((pair_ref, first), (pair_ref, second), (grad_ref, first), (grad_ref, second))
         ):
@@ -134,6 +152,23 @@
                     sections - 1, host,
                 )
 
+    def go_low():
+        go(s - half + 1)
+
+    def go(section):
+        pl.semaphore_signal(go_sem, inc=1, device_id=(section, d), device_id_type=MESH)
+
+    def sent(a):
+        if chained:
+            @pl.when(early if a == order[0] else both(splits, jnp.logical_not(early)))
+            def _():
+                go_low()
+
+            if a == order[1]:
+                @pl.when(odd)
+                def _():
+                    go(s - 1)
+
     def weights_out():
         if chained:
             @pl.when(follows)
@@ -149,44 +184,85 @@
                         send(owns[a], shard(a, d), w_send.at[a], w_recv.at[a], s, t)
             for a in order:
                 fulls[a][pl.ds(pl.multiple_of(d * part, part), part), :] = owns[a][...]
-            if m > 1:
-                for a in order:
-                    wait_bytes(fulls[a].at[pl.ds(0, (m - 1) * part)], w_send.at[a])
-
-        @pl.when(is_mate)
-        def _():
             for a in order:
                 if m > 1:
+                    wait_bytes(fulls[a].at[pl.ds(0, (m - 1) * part)], w_send.at[a])
+                sent(a)
+
+        @pl.when(is_mate)
+        def _():
+            for a in order:
+                if m > 1:
+                    size = part // pieces
                     for c in range(pieces):
-                        size = part // pieces
                         rows = pl.ds(c * size, size)
-                        send(
-                            owns[a].at[rows], relay.at[a, rows], w_send.at[a], r_recv.at[a, c],
-                            partner, d,
-                        )
+                        relayed = True if c < pieces // 2 else jnp.logical_not(halves)
+
+                        @pl.when(relayed)
+                        def _():
+                            send(
+                                owns[a].at[rows], relay.at[a, rows], w_send.at[a],
+                                r_recv.at[a, c], partner, d,
+                            )
                 send(owns[a], shard(a, d), w_send.at[a], w_recv.at[a], s, host)
+                if m > 1:
+                    @pl.when(halves)
+                    def _():
+                        lead = part // 2
+                        for t in hosts:
+                            @pl.when(host != t)
+                            def _():
+                                send(
+                                    owns[a].at[pl.ds(lead, lead)], shard(a, d, lead, lead),
+                                    w_send.at[a], w_recv.at[a], s, t,
+                                )
             for a in order:
-                wait_bytes(fulls[a].at[pl.ds(0, (2 if m > 1 else 1) * part)], w_send.at[a])
-
-        if chained:
-            @pl.when(leads)
-            def _():
-                pl.semaphore_signal(go_sem, inc=1, device_id=(follower, d), device_id_type=MESH)
+                if m > 1:
+                    @pl.when(halves)
+                    def _():
+                        lead = part // 2
+                        wait_bytes(fulls[a].at[pl.ds(0, part + m * lead)], w_send.at[a])
+
+                    @pl.when(jnp.logical_not(halves))
+                    def _():
+                        wait_bytes(fulls[a].at[pl.ds(0, 2 * part)], w_send.at[a])
+                else:
+                    wait_bytes(fulls[a].at[pl.ds(0, part)], w_send.at[a])
+                sent(a)
 
     def pass_on():
         if m > 1:
+            size = part // pieces
             for a in order:
                 for c in range(pieces):
-                    size = part // pieces
                     rows = pl.ds(c * size, size)
-                    wait_bytes(relay.at[a, rows], r_recv.at[a, c])
-                    for t in hosts:
-                        @pl.when(host != t)
-                        def _():
-                            send(
-                                relay.at[a, rows], shard(a, d, c * size, size), r_send,
-                                w_recv.at[a], partner, t,
-                            )
+                    relayed = True if c < pieces // 2 else jnp.logical_not(splits)
+
+                    @pl.when(relayed)
+                    def _():
+                        wait_bytes(relay.at[a, rows], r_recv.at[a, c])
+                        for t in hosts:
+                            @pl.when(host != t)
+                            def _():
+                                send(
+                                    relay.at[a, rows], shard(a, d, c * size, size), r_send,
+                                    w_recv.at[a], partner, t,
+                                )
+
+    def passed_on():
+        if m > 1:
+            @pl.when(splits)
+            def _():
+                for k in range(m - 1):
+                    wait_bytes(relay.at[0], r_send)
+
+            @pl.when(jnp.logical_not(splits))
+            def _():
+                for k in range(m - 1):
+                    wait_bytes(relay, r_send)
+
+    def clear(section):
+        pl.semaphore_signal(clear_sem, inc=1, device_id=(section, host), device_id_type=MESH)
 
     @pl.when(both(is_mate, low))
     def _():
@@ -194,9 +270,22 @@
 
     weights_out()
 
+    @pl.when(feeds)
+    def _():
+        feed()
+
     @pl.when(both(is_mate, high))
     def _():
         pass_on()
+        passed_on()
+
+        if chained:
+            @pl.when(even)
+            def _():
+                clear(s)
+                clear(s + 1)
+        else:
+            clear(s)
 
     def take(i, b, rows, source, column):
         local = both(is_last, b < own_blocks)
@@ -240,7 +329,8 @@
                     d_send.at[a], d_recv.at[a], s, t,
                 )
 
-    def block(b, carry):
+    def block(step, carry):
+        b = place_of(step)
         rows = block_rows(b)
         is_own = b < own_blocks
         gain_f, gain_g = gains_ref[0:1, :], gains_ref[1:2, :]
@@ -263,7 +353,7 @@
         r2 = inverse_scale(x2)
         norm_f = (x2 * r2 * gain_f).astype(bf16)
 
-        @pl.when(b == 0)
+        @pl.when(step == 0)
         def _():
             wait_bytes(wf.at[pl.ds(0, (n - 1) * part)], w_recv.at[0])
 
@@ -281,12 +371,14 @@
             norms_own[0, e, rows] = norm_f[:, e * part:(e + 1) * part]
             norms_own[1, e, rows] = norm_g[:, e * part:(e + 1) * part]
 
-        @pl.when(low)
+        streams = both(low, jnp.logical_not(both(holds, step < blocks // 2)))
+
+        @pl.when(streams)
         def _():
             share_norm(1, rows)
             share_norm(0, rows)
 
-        @pl.when(b == 0)
+        @pl.when(step == 0)
         def _():
             wgt[...] = wg[...].T
             wft[...] = wf[...].T
@@ -297,7 +389,7 @@
         back_g = jnp.dot(delta_g, wgt[...], preferred_element_type=f32)
         deltas[1, pair_index, rows] = delta_g
 
-        @pl.when(low)
+        @pl.when(streams)
         def _():
             share_delta(1, rows)
 
@@ -317,10 +409,6 @@
         back_f = jnp.dot(delta_f, wft[...], preferred_element_type=f32)
         deltas[0, pair_index, rows] = delta_f
 
-        @pl.when(low)
-        def _():
-            share_delta(0, rows)
-
         x2 = held[1]
         weighted = gain_f * back_f
         gx2 = held[3] + r2 * weighted - x2 * (r2 * r2 * r2) * jnp.mean(
@@ -352,9 +440,23 @@
 
         @pl.when(high)
         def _():
+            pl.semaphore_wait(clear_sem, 1)
             for a in order:
                 share_norm(a, whole)
                 share_delta(a, whole)
+
+        @pl.when(holds)
+        def _():
+            for step in range(blocks // 2):
+                place = 0 if step == 0 else step - 1 + own_blocks
+                rows = pl.ds(place * rows_per, rows_per)
+                share_norm(1, rows)
+                share_delta(1, rows)
+                share_norm(0, rows)
+
+        @pl.when(low)
+        def _():
+            share_delta(0, whole)
 
         gain_parts[pair_index] = gain_acc[...]
         for k in range(1, n):
@@ -420,11 +522,9 @@
         def _():
             wait_bytes(tx, p_send)
 
-    if m > 1:
-        @pl.when(is_mate)
-        def _():
-            for k in range(m - 1):
-                wait_bytes(relay, r_send)
+    @pl.when(both(is_mate, low))
+    def _():
+        passed_on()
 
     @pl.when(feeds)
     def _():
@@ -436,7 +536,7 @@
     tokens, width = out_pair.shape
     h = width // 2
     part = f_weight.shape[1]
-    blocks = 4
+    blocks = 8
     m = n // 2
     rows_all = 2 * tokens
     vmem = pl.BlockSpec(memory_space=pltpu.VMEM)
@@ -470,10 +570,11 @@
             pltpu.VMEM((2, h), f32),
             pltpu.VMEM((n, 2, h), f32),
             pltpu.SemaphoreType.REGULAR,
+            pltpu.SemaphoreType.REGULAR,
             dma((2,)),
             dma((2,)),
             dma,
-            dma((2, 2)),
+            dma((2, 4)),
             dma,
             dma,
             dma((4, blocks)),

time: 149 us -> 132 us (0.89)
  Pallas kernels: 142 us -> 125 us
    pallas_call x1, Pallas kernels: 142 us -> 125 us  [shards(): pl.pallas_call(functools.partial(kernel, n, sections, blocks), out_shape=...]
where the time goes in v2:
time: 132 us
  Pallas kernels  125 us (95%)
  local copies, waits for them, and re-layouts  6.39 us (5%)
    pallas_call x1, Pallas kernels, shards(): pl.pallas_call(functools.partial(kernel, n, sections, blocks), out_shape=...  125 us
    unnamed x13, local copies, waits for them, and re-layouts  6.39 us

profile of v2, /device:TPU:0, one launch (start us, length us, event | category | flops | bytes accessed | tf_op | source)
XLA Modules:
  0.0 131.8 jit_solution(18411171172087492771)
XLA Ops:
  0.6 124.8 %shard_map.92 = (f32[128,2048]{1,0:T(8,128)}, bf16[128,2048]{1,0:T(8,128)(2,1)}, f32[256,1024]{1,0:T(8,128)}, f32[256,1024]{1,0:T(8,128)}, f32[2,1024]{1,0:T(2,128)}) custom-call(f32[128,2048]{1,0:T(8,128)} %pair_ref.1, bf16[128,2048]{1,0:T(8,128)(2,1)} %grad_ref.1, bf16[256,1024]{1,0:T(8,128)(2,1)} %bitcast.11, bf16[256,1024]{1,0:T(8,128)(2,1)} %bitcast.12, ...), custom_call_target="tpu_custom_call" | custom-call | tf_op jit(solution)/shard_map/pallas_call | solution.py:544
  125.4 0.0 copy-start.2
  125.4 0.0 copy-start.1
  125.4 2.4 %copy.15 = f32[1,128,2048]{2,1,0:T(8,128)} copy(f32[1,128,2048]{2,1,0:T(8,128)} %bitcast.10) | data formatting | bytes 2097152
  127.8 0.0 copy-done.2
  127.8 0.8 copy.16
  128.6 0.0 copy-done.1
  128.6 0.0 copy-start
  128.6 1.0 copy.17
  129.6 0.6 copy-done
  130.2 0.0 copy-start.3
  130.2 1.0 copy.18
  131.2 0.0 copy-done.3
  131.2 0.6 copy.19
Async XLA Ops:
  125.4 2.4 %copy-start.2 = (bf16[128,2048]{1,0:T(8,128)(2,1)S(1)}, bf16[128,2048]{1,0:T(8,128)(2,1)}, u32[]{:S(2)}) copy-start(bf16[128,2048]{1,0:T(8,128)(2,1)} %get-tuple-element.11) | copy-start | bytes 1572868
  125.4 3.2 %copy-start.1 = (f32[256,1024]{1,0:T(8,128)S(1)}, f32[256,1024]{1,0:T(8,128)}, u32[]{:S(2)}) copy-start(f32[256,1024]{1,0:T(8,128)} %get-tuple-element.12) | copy-start | bytes 3145732
  128.6 1.6 %copy-start = (f32[256,1024]{1,0:T(8,128)S(1)}, f32[256,1024]{1,0:T(8,128)}, u32[]{:S(2)}) copy-start(f32[256,1024]{1,0:T(8,128)} %get-tuple-element.13) | copy-start | bytes 3145732
  130.2 1.0 copy-start.3

commit v3 on v2

--- a/solution.py
+++ b/solution.py
@@ -25,9 +25,9 @@
     n, sections, blocks,
     pair_ref, grad_ref, fw_ref, gw_ref, gains_ref,
     in_pair_ref, in_grad_ref, f_out, g_out, gain_out,
-    wf, wg, wft, wgt, relay, rx, tx, held, slopes, norms_own, norms, deltas, result_tx, result_rx, gain_acc, gain_parts,
+    wf, wg, wft, wgt, relay, rx, tx, held, slopes, norms_own, norms, deltas, result_tx, result_rx, gain_acc, gain_parts, via, delta_via,
     go_sem, clear_sem, w_send, w_recv, r_send, r_recv, feed_send,
-    p_send, p_recv, m_send, m_recv, n_send, n_recv, d_send, d_recv, c_send, c_recv, e_send, e_recv,
+    p_send, p_recv, m_send, m_recv, n_send, n_recv, d_send, d_recv, c_send, c_recv, e_send, e_recv, v_send, v_recv, y_send, y_recv,
 ):
     s, d = lax.axis_index("section"), lax.axis_index("dp")
     m = n // 2
@@ -58,8 +58,11 @@
     follows = jnp.logical_not(both(odd, high))
     splits = both(even, high)
     halves = both(even, low)
-    holds = both(both(odd, low), s > 1)
     early = both(splits, s < sections - 2)
+    waits = both(high, s >= sections - 2) if chained else high
+    holds = jnp.logical_not(waits) & (high | both(odd, s > 1))
+    routed = s < 2
+    routes = both(high, s - half < 2)
     feeder = max(sections - 3, 0)
     feeds = both(s == feeder, is_mate)
     is_fed = both(is_last, is_host)
@@ -118,6 +121,7 @@
     order = (1, 0)
     pieces = 4
     first, second = pl.ds(0, h), pl.ds(h, h)
+    every = pl.ds(0, h)
 
     def wait_bytes(ref, sem):
         pltpu.make_async_copy(ref, ref, sem).wait()
@@ -280,7 +284,7 @@
         passed_on()
 
         if chained:
-            @pl.when(even)
+            @pl.when(both(even, s >= sections - 2))
             def _():
                 clear(s)
                 clear(s + 1)
@@ -320,14 +324,35 @@
                     n_send.at[a], n_recv.at[a], s, t,
                 )
 
-    def share_delta(a, rows):
+    def share_delta(a, rows, cols, slot):
         for t in hosts:
             @pl.when(d != t)
             def _():
                 send(
-                    deltas.at[a, pair_index, rows], deltas.at[a, pair_index, rows],
-                    d_send.at[a], d_recv.at[a], s, t,
+                    deltas.at[a, pair_index, rows, cols], deltas.at[a, pair_index, rows, cols],
+                    d_send.at[slot], d_recv.at[slot], s, t,
                 )
+
+    left = pl.ds(0, via.shape[1])
+    ways = ((1, every, 2), (0, left, 0), (0, pl.ds(left.size, h - left.size), 1))
+
+    def route_delta(step, rows):
+        send(
+            deltas.at[0, pair_index, rows, left], delta_via.at[rows], d_send.at[0],
+            y_recv.at[step], partner, host,
+        )
+
+    def forward(step, carry):
+        rows = block_rows(place_of(step))
+        wait_bytes(delta_via.at[rows], y_recv.at[step])
+        for t in hosts:
+            @pl.when(d != t)
+            def _():
+                send(
+                    delta_via.at[rows], deltas.at[0, pair_index, rows, left],
+                    y_send, d_recv.at[0], partner, t,
+                )
+        return carry
 
     def block(step, carry):
         b = place_of(step)
@@ -371,7 +396,16 @@
             norms_own[0, e, rows] = norm_f[:, e * part:(e + 1) * part]
             norms_own[1, e, rows] = norm_g[:, e * part:(e + 1) * part]
 
-        streams = both(low, jnp.logical_not(both(holds, step < blocks // 2)))
+        streams = jnp.logical_not(waits | both(holds, step < blocks // 2))
+
+        @pl.when(both(holds, step == blocks // 2))
+        def _():
+            for earlier in range(blocks // 2):
+                place = 0 if earlier == 0 else earlier - 1 + own_blocks
+                held_rows = pl.ds(place * rows_per, rows_per)
+                share_norm(1, held_rows)
+                share_delta(1, held_rows, every, 2)
+                share_norm(0, held_rows)
 
         @pl.when(streams)
         def _():
@@ -391,7 +425,7 @@
 
         @pl.when(streams)
         def _():
-            share_delta(1, rows)
+            share_delta(1, rows, every, 2)
 
         y1 = held[0]
         weighted = gain_g * back_g
@@ -409,6 +443,10 @@
         back_f = jnp.dot(delta_f, wft[...], preferred_element_type=f32)
         deltas[0, pair_index, rows] = delta_f
 
+        @pl.when(routed)
+        def _():
+            route_delta(step, rows)
+
         x2 = held[1]
         weighted = gain_f * back_f
         gx2 = held[3] + r2 * weighted - x2 * (r2 * r2 * r2) * jnp.mean(
@@ -426,9 +464,10 @@
     whole = pl.ds(0, rows_all)
     outs = (f_out, g_out)
 
-    def product(a, which):
+    def product(a, which, cols):
         return lax.dot_general(
-            norms[a, which].reshape(m * rows_all, part), deltas[a].reshape(m * rows_all, h),
+            norms[a, which].reshape(m * rows_all, part),
+            deltas[a, :, :, cols].reshape(m * rows_all, cols.size),
             (((0,), (0,)), ((), ())), preferred_element_type=f32,
         )
 
@@ -438,25 +477,22 @@
         wait_bytes(wg.at[pl.ds(0, (n - 1) * part)], w_recv.at[1])
         lax.fori_loop(0, blocks, block, 0)
 
-        @pl.when(high)
+        @pl.when(waits)
         def _():
             pl.semaphore_wait(clear_sem, 1)
-            for a in order:
-                share_norm(a, whole)
-                share_delta(a, whole)
-
-        @pl.when(holds)
-        def _():
-            for step in range(blocks // 2):
-                place = 0 if step == 0 else step - 1 + own_blocks
-                rows = pl.ds(place * rows_per, rows_per)
-                share_norm(1, rows)
-                share_delta(1, rows)
-                share_norm(0, rows)
-
-        @pl.when(low)
-        def _():
-            share_delta(0, whole)
+            share_norm(1, whole)
+            share_delta(*ways[0][:1], whole, *ways[0][1:])
+            share_norm(0, whole)
+            for a, cols, slot in ways[1:]:
+                share_delta(a, whole, cols, slot)
+
+        @pl.when(jnp.logical_not(waits | routed))
+        def _():
+            share_delta(*ways[1][:1], whole, *ways[1][1:])
+
+        @pl.when(jnp.logical_not(waits))
+        def _():
+            share_delta(*ways[2][:1], whole, *ways[2][1:])
 
         gain_parts[pair_index] = gain_acc[...]
         for k in range(1, n):
@@ -467,14 +503,50 @@
         for a in range(2):
             for w in range(2):
                 norms[a, w, pair_index] = norms_own[a, 2 * pair_index + w]
+        for a, cols, slot in ways:
+            if m > 1:
+                if slot != 1:
+                    wait_bytes(norms.at[a, pl.ds(0, 2), pl.ds(0, m - 1)], n_recv.at[a])
+                wait_bytes(deltas.at[a, pl.ds(0, m - 1), whole, cols], d_recv.at[slot])
+            result_tx[a, :, cols] = product(a, parity, cols).astype(bf16)
+
+            def direct():
+                send(
+                    result_tx.at[a, :, cols], result_rx.at[a, :, cols], e_send.at[slot],
+                    e_recv.at[slot], s, mate,
+                )
+
+            if slot == 0:
+                @pl.when(high)
+                def _():
+                    direct()
+
+                @pl.when(low)
+                def _():
+                    for c in range(2):
+                        lines = pl.ds(c * (part // 2), part // 2)
+                        send(
+                            result_tx.at[a, lines, cols], via.at[lines], e_send.at[slot],
+                            v_recv.at[c], partner, host,
+                        )
+            else:
+                direct()
         for a in order:
-            if m > 1:
-                wait_bytes(norms.at[a, pl.ds(0, 2), pl.ds(0, m - 1)], n_recv.at[a])
-                wait_bytes(deltas.at[a, pl.ds(0, m - 1)], d_recv.at[a])
-            result_tx[a] = product(a, parity).astype(bf16)
-            send(result_tx.at[a], result_rx.at[a], e_send.at[a], e_recv.at[a], s, mate)
-        for a in order:
-            outs[a][...] = product(a, 1 - parity)
+            outs[a][...] = product(a, 1 - parity, every)
+
+        @pl.when(routes)
+        def _():
+            lax.fori_loop(0, blocks, forward, 0)
+
+        @pl.when(high)
+        def _():
+            for c in range(2):
+                lines = pl.ds(c * (part // 2), part // 2)
+                wait_bytes(via.at[lines], v_recv.at[c])
+                send(
+                    via.at[lines], result_rx.at[0, lines, left], v_send, e_recv.at[0],
+                    partner, mate,
+                )
 
     @pl.when(is_mate)
     def _():
@@ -490,9 +562,9 @@
             return carry
 
         lax.fori_loop(0, own_blocks, collect, 0)
-        for a in order:
-            wait_bytes(result_rx.at[a], e_recv.at[a])
-            outs[a][...] = result_rx[a].astype(f32)
+        for a, cols, slot in (ways[0], ways[2], ways[1]):
+            wait_bytes(result_rx.at[a, :, cols], e_recv.at[slot])
+            outs[a][:, cols] = result_rx[a, :, cols].astype(f32)
 
     @pl.when(is_mate)
     def _():
@@ -511,11 +583,32 @@
     @pl.when(is_host)
     def _():
         wait_bytes(gain_parts.at[pl.ds(0, n - 1)], c_send)
-        for a in range(2):
-            wait_bytes(result_tx.at[a], e_send.at[a])
+        for a, cols, slot in ways:
+            wait_bytes(result_tx.at[a, :, cols], e_send.at[slot])
             if m > 1:
-                wait_bytes(norms.at[a, pl.ds(0, 2), pl.ds(0, m - 1)], n_send.at[a])
-                wait_bytes(deltas.at[a, pl.ds(0, m - 1)], d_send.at[a])
+                if slot != 1:
+                    wait_bytes(norms.at[a, pl.ds(0, 2), pl.ds(0, m - 1)], n_send.at[a])
+                if slot == 0:
+                    @pl.when(jnp.logical_not(routed))
+                    def _():
+                        wait_bytes(deltas.at[0, pl.ds(0, m - 1), whole, left], d_send.at[0])
+                else:
+                    wait_bytes(deltas.at[a, pl.ds(0, m - 1), whole, cols], d_send.at[slot])
+
+        @pl.when(routed)
+        def _():
+            wait_bytes(delta_via, d_send.at[0])
+
+        @pl.when(high)
+        def _():
+            wait_bytes(via, v_send)
+
+        if m > 1:
+            @pl.when(routes)
+            def _():
+                for k in range(m - 1):
+                    wait_bytes(delta_via, y_send)
+
         wait_bytes(tx.at[:, pl.ds(0, tokens)], m_send)
 
         @pl.when(has_below)
@@ -529,6 +622,16 @@
     @pl.when(feeds)
     def _():
         wait_bytes(tx.at[:, pl.ds(0, tokens)], feed_send)
+
+
+def put(*refs):
+    k = len(refs) // 2
+    sems = refs[-1]
+    copies = [pltpu.make_async_copy(refs[i], refs[k + i], sems.at[i]) for i in range(k)]
+    for copy in copies:
+        copy.start()
+    for copy in copies:
+        copy.wait()
 
 
 def shards(out_pair, out_grad, f_weight, g_weight, gains):
@@ -539,6 +642,7 @@
     blocks = 8
     m = n // 2
     rows_all = 2 * tokens
+    split = h // 2
     vmem = pl.BlockSpec(memory_space=pltpu.VMEM)
     dma = pltpu.SemaphoreType.DMA
     outs = pl.pallas_call(
@@ -569,6 +673,8 @@
             pltpu.VMEM((2, part, h), bf16),
             pltpu.VMEM((2, h), f32),
             pltpu.VMEM((n, 2, h), f32),
+            pltpu.VMEM((part, split), bf16),
+            pltpu.VMEM((rows_all, split), bf16),
             pltpu.SemaphoreType.REGULAR,
             pltpu.SemaphoreType.REGULAR,
             dma((2,)),
@@ -582,17 +688,29 @@
             dma((4, blocks)),
             dma((2,)),
             dma((2,)),
-            dma((2,)),
+            dma((3,)),
+            dma((3,)),
+            dma,
+            dma,
+            dma((3,)),
+            dma((3,)),
+            dma,
             dma((2,)),
             dma,
-            dma,
-            dma((2,)),
-            dma((2,)),
+            dma((blocks,)),
         ],
         compiler_params=pltpu.CompilerParams(
             collective_id=0, has_side_effects=True, vmem_limit_bytes=60 * 1024 * 1024
         ),
     )(out_pair, out_grad, f_weight[0], g_weight[0], gains[0])
+    outs = pl.pallas_call(
+        put,
+        out_shape=tuple(jax.ShapeDtypeStruct(out.shape, out.dtype) for out in outs),
+        in_specs=[vmem] * 5,
+        out_specs=[pl.BlockSpec(memory_space=pl.ANY)] * 5,
+        scratch_shapes=[dma((5,))],
+        compiler_params=pltpu.CompilerParams(has_side_effects=False),
+    )(*outs)
     return tuple(out[None] for out in outs)
 
 

time: 132 us -> 124 us (0.939)
  local copies, waits for them, and re-layouts: 6.39 us -> 0 us
  Pallas kernels: 125 us -> 123 us
    unnamed x13 -> x0, local copies, waits for them, and re-layouts: 6.39 us -> none
    pallas_call x1, Pallas kernels: 125 us -> 119 us  [shards(): pl.pallas_call(functools.partial(kernel, n, sections, blocks), out_shape=...]
    pallas_call x0 -> x1, Pallas kernels: none -> 3.9 us  [shards(): pl.pallas_call(put, out_shape=tuple((jax.ShapeDtypeStruct(out.shape, out....]
where the time goes in v3:
time: 124 us
  Pallas kernels  123 us (99%)
    pallas_call x1, Pallas kernels, shards(): pl.pallas_call(functools.partial(kernel, n, sections, blocks), out_shape=...  119 us
    pallas_call x1, Pallas kernels, shards(): pl.pallas_call(put, out_shape=tuple((jax.ShapeDtypeStruct(out.shape, out....  3.9 us

profile of v3, /device:TPU:0, one launch (start us, length us, event | category | flops | bytes accessed | tf_op | source)
XLA Modules:
  0.0 123.9 jit_solution(7422540535173545811)
XLA Ops:
  0.6 119.3 %shard_map.92 = (f32[128,2048]{1,0:T(8,128)}, bf16[128,2048]{1,0:T(8,128)(2,1)}, f32[256,1024]{1,0:T(8,128)}, f32[256,1024]{1,0:T(8,128)}, f32[2,1024]{1,0:T(2,128)}) custom-call(f32[128,2048]{1,0:T(8,128)} %pair_ref.1, bf16[128,2048]{1,0:T(8,128)(2,1)} %grad_ref.1, bf16[256,1024]{1,0:T(8,128)(2,1)} %bitcast.8, bf16[256,1024]{1,0:T(8,128)(2,1)} %bitcast.9, ...), custom_call_target="tpu_custom_call" | custom-call | tf_op jit(solution)/shard_map/pallas_call | solution.py:648
  120.0 3.9 %shard_map.93 = (f32[128,2048]{1,0:T(8,128)}, bf16[128,2048]{1,0:T(8,128)(2,1)}, f32[256,1024]{1,0:T(8,128)}, f32[256,1024]{1,0:T(8,128)}, f32[2,1024]{1,0:T(2,128)}) custom-call(f32[128,2048]{1,0:T(8,128)} %get-tuple-element.15.refs_0_, bf16[128,2048]{1,0:T(8,128)(2,1)} %get-tuple-element.16.refs_1_, f32[256,1024]{1,0:T(8,128)} %get-tuple-element.17.refs_2_, ...), custom_call_target="tpu_custom_call" | custom-call | tf_op jit(solution)/shard_map/pallas_call | solution.py:706

commit v4 on v3

--- a/solution.py
+++ b/solution.py
@@ -23,13 +23,29 @@
 
 def kernel(
     n, sections, blocks,
-    pair_ref, grad_ref, fw_ref, gw_ref, gains_ref,
-    in_pair_ref, in_grad_ref, f_out, g_out, gain_out,
-    wf, wg, wft, wgt, relay, rx, tx, held, slopes, norms_own, norms, deltas, result_tx, result_rx, gain_acc, gain_parts, via, delta_via,
+    pair_in, grad_in, fw_in, gw_in, gains_in,
+    in_pair_out, in_grad_out, f_put, g_put, gain_out,
+    pair_ref, grad_ref, fw_ref, gw_ref, gains_ref, in_pair_ref, in_grad_ref, f_out, g_out,
+    wf, wg, wft, wgt, relay, rx, tx, held, slopes, norms_own, norms, deltas, result_tx, result_rx, gain_acc, gain_parts, via, delta_via, g_via,
     go_sem, clear_sem, w_send, w_recv, r_send, r_recv, feed_send,
-    p_send, p_recv, m_send, m_recv, n_send, n_recv, d_send, d_recv, c_send, c_recv, e_send, e_recv, v_send, v_recv, y_send, y_recv,
+    p_send, p_recv, m_send, m_recv, n_send, n_recv, d_send, d_recv, c_send, c_recv, e_send, e_recv, v_send, v_recv, y_send, y_recv, l_sem, o_sem,
 ):
     s, d = lax.axis_index("section"), lax.axis_index("dp")
+    loads = [
+        pltpu.make_async_copy(source, target, l_sem.at[i])
+        for i, (source, target) in enumerate((
+            (gw_in, gw_ref), (fw_in, fw_ref), (pair_in, pair_ref), (grad_in, grad_ref),
+            (gains_in, gains_ref),
+        ))
+    ]
+    for load in loads:
+        load.start()
+    puts = [
+        pltpu.make_async_copy(source, target, o_sem.at[i])
+        for i, (source, target) in enumerate((
+            (f_out, f_put), (g_out, g_put), (in_pair_ref, in_pair_out), (in_grad_ref, in_grad_out),
+        ))
+    ]
     m = n // 2
     half = sections // 2
     tokens = pair_ref.shape[0]
@@ -115,6 +131,8 @@
             greet(s - 1, mate)
 
         neighbours += both(high, both(even, is_mate) | both(odd, is_host)).astype(jnp.int32)
+    for load in loads:
+        load.wait()
     pl.semaphore_wait(barrier, neighbours)
 
     fulls, owns = (wf, wg), (fw_ref, gw_ref)
@@ -476,6 +494,8 @@
         gain_acc[...] = jnp.zeros_like(gain_acc)
         wait_bytes(wg.at[pl.ds(0, (n - 1) * part)], w_recv.at[1])
         lax.fori_loop(0, blocks, block, 0)
+        puts[2].start()
+        puts[3].start()
 
         @pl.when(waits)
         def _():
@@ -516,7 +536,27 @@
                     e_recv.at[slot], s, mate,
                 )
 
-            if slot == 0:
+            if slot == 2:
+                head, end = pl.ds(0, part - g_via.shape[0]), pl.ds(part - g_via.shape[0], g_via.shape[0])
+                send(
+                    result_tx.at[1, head], result_rx.at[1, head], e_send.at[slot],
+                    e_recv.at[slot], s, mate,
+                )
+
+                @pl.when(high)
+                def _():
+                    send(
+                        result_tx.at[1, end], result_rx.at[1, end], e_send.at[slot],
+                        e_recv.at[slot], s, mate,
+                    )
+
+                @pl.when(low)
+                def _():
+                    send(
+                        result_tx.at[1, end], g_via, e_send.at[slot], v_recv.at[2],
+                        partner, host,
+                    )
+            elif slot == 0:
                 @pl.when(high)
                 def _():
                     direct()
@@ -533,6 +573,7 @@
                 direct()
         for a in order:
             outs[a][...] = product(a, 1 - parity, every)
+            puts[a].start()
 
         @pl.when(routes)
         def _():
@@ -540,11 +581,14 @@
 
         @pl.when(high)
         def _():
+            wait_bytes(g_via, v_recv.at[2])
+            end = pl.ds(part - g_via.shape[0], g_via.shape[0])
+            send(g_via, result_rx.at[1, end], v_send.at[1], e_recv.at[2], partner, mate)
             for c in range(2):
                 lines = pl.ds(c * (part // 2), part // 2)
                 wait_bytes(via.at[lines], v_recv.at[c])
                 send(
-                    via.at[lines], result_rx.at[0, lines, left], v_send, e_recv.at[0],
+                    via.at[lines], result_rx.at[0, lines, left], v_send.at[0], e_recv.at[0],
                     partner, mate,
                 )
 
@@ -562,9 +606,13 @@
             return carry
 
         lax.fori_loop(0, own_blocks, collect, 0)
+        puts[2].start()
+        puts[3].start()
         for a, cols, slot in (ways[0], ways[2], ways[1]):
             wait_bytes(result_rx.at[a, :, cols], e_recv.at[slot])
             outs[a][:, cols] = result_rx[a, :, cols].astype(f32)
+            if slot != 1:
+                puts[a].start()
 
     @pl.when(is_mate)
     def _():
@@ -601,7 +649,8 @@
 
         @pl.when(high)
         def _():
-            wait_bytes(via, v_send)
+            wait_bytes(via, v_send.at[0])
+            wait_bytes(g_via, v_send.at[1])
 
         if m > 1:
             @pl.when(routes)
@@ -623,15 +672,34 @@
     def _():
         wait_bytes(tx.at[:, pl.ds(0, tokens)], feed_send)
 
-
-def put(*refs):
-    k = len(refs) // 2
-    sems = refs[-1]
-    copies = [pltpu.make_async_copy(refs[i], refs[k + i], sems.at[i]) for i in range(k)]
-    for copy in copies:
-        copy.start()
-    for copy in copies:
-        copy.wait()
+    for put in puts:
+        put.wait()
+
+
+def put(k, *refs):
+    sources, targets, held = refs[:k], refs[k:2 * k], refs[2 * k:3 * k]
+    in_sem, out_sem = refs[3 * k:]
+    halves = []
+    for i in range(k):
+        rows = sources[i].shape[0]
+        pieces = 2 if rows % 32 == 0 else 1
+        for c in range(pieces):
+            lines = pl.ds(c * (rows // pieces), rows // pieces)
+            halves.append((
+                pltpu.make_async_copy(
+                    sources[i].at[lines], held[i].at[lines], in_sem.at[i, c]
+                ),
+                pltpu.make_async_copy(
+                    held[i].at[lines], targets[i].at[lines], out_sem.at[i, c]
+                ),
+            ))
+    for taken, _ in halves:
+        taken.start()
+    for taken, given in halves:
+        taken.wait()
+        given.start()
+    for _, given in halves:
+        given.wait()
 
 
 def shards(out_pair, out_grad, f_weight, g_weight, gains):
@@ -643,7 +711,7 @@
     m = n // 2
     rows_all = 2 * tokens
     split = h // 2
-    vmem = pl.BlockSpec(memory_space=pltpu.VMEM)
+    vmem, anywhere = pl.BlockSpec(memory_space=pltpu.VMEM), pl.BlockSpec(memory_space=pl.ANY)
     dma = pltpu.SemaphoreType.DMA
     outs = pl.pallas_call(
         functools.partial(kernel, n, sections, blocks),
@@ -654,9 +722,18 @@
             jax.ShapeDtypeStruct((part, h), f32),
             jax.ShapeDtypeStruct((2, h), f32),
         ),
-        in_specs=[vmem] * 5,
-        out_specs=[vmem] * 5,
+        in_specs=[anywhere] * 5,
+        out_specs=[anywhere] * 4 + [vmem],
         scratch_shapes=[
+            pltpu.VMEM((tokens, width), f32),
+            pltpu.VMEM((tokens, width), bf16),
+            pltpu.VMEM((part, h), bf16),
+            pltpu.VMEM((part, h), bf16),
+            pltpu.VMEM((2, h), f32),
+            pltpu.VMEM((tokens, width), f32),
+            pltpu.VMEM((tokens, width), bf16),
+            pltpu.VMEM((part, h), f32),
+            pltpu.VMEM((part, h), f32),
             pltpu.VMEM((h, h), bf16),
             pltpu.VMEM((h, h), bf16),
             pltpu.VMEM((h, h), bf16),
@@ -675,6 +752,7 @@
             pltpu.VMEM((n, 2, h), f32),
             pltpu.VMEM((part, split), bf16),
             pltpu.VMEM((rows_all, split), bf16),
+            pltpu.VMEM((part // 4, h), bf16),
             pltpu.SemaphoreType.REGULAR,
             pltpu.SemaphoreType.REGULAR,
             dma((2,)),
@@ -694,22 +772,28 @@
             dma,
             dma((3,)),
             dma((3,)),
-            dma,
             dma((2,)),
+            dma((3,)),
             dma,
             dma((blocks,)),
+            dma((5,)),
+            dma((4,)),
         ],
         compiler_params=pltpu.CompilerParams(
             collective_id=0, has_side_effects=True, vmem_limit_bytes=60 * 1024 * 1024
         ),
     )(out_pair, out_grad, f_weight[0], g_weight[0], gains[0])
     outs = pl.pallas_call(
-        put,
+        functools.partial(put, len(outs)),
         out_shape=tuple(jax.ShapeDtypeStruct(out.shape, out.dtype) for out in outs),
-        in_specs=[vmem] * 5,
-        out_specs=[pl.BlockSpec(memory_space=pl.ANY)] * 5,
-        scratch_shapes=[dma((5,))],
-        compiler_params=pltpu.CompilerParams(has_side_effects=False),
+        in_specs=[anywhere] * len(outs),
+        out_specs=[anywhere] * len(outs),
+        scratch_shapes=[
+            *(pltpu.VMEM(out.shape, out.dtype) for out in outs),
+            dma((len(outs), 2)),
+            dma((len(outs), 2)),
+        ],
+        compiler_params=pltpu.CompilerParams(vmem_limit_bytes=60 * 1024 * 1024),
     )(*outs)
     return tuple(out[None] for out in outs)
 

time: 124 us -> 121 us (0.976)
  Pallas kernels: 123 us -> 120 us
    pallas_call x1, Pallas kernels: 119 us -> 117 us  [shards(): pl.pallas_call(functools.partial(kernel, n, sections, blocks), out_shape=...]
where the time goes in v4:
time: 121 us; the launch traced here: 120 us
  Pallas kernels  120 us (99%)
    pallas_call x1, Pallas kernels, shards(): pl.pallas_call(functools.partial(kernel, n, sections, blocks), out_shape=...  117 us
    pallas_call x1, Pallas kernels, shards(): pl.pallas_call(functools.partial(put, len(outs)), out_shape=tuple((jax.Sh...  3.08 us

profile of v4, /device:TPU:0, one launch (start us, length us, event | category | flops | bytes accessed | tf_op | source)
XLA Modules:
  0.0 120.4 jit_solution(212062603239065474)
XLA Ops:
  0.6 116.7 %shard_map.92 = (f32[128,2048]{1,0:T(8,128)}, bf16[128,2048]{1,0:T(8,128)(2,1)}, f32[256,1024]{1,0:T(8,128)}, f32[256,1024]{1,0:T(8,128)}, f32[2,1024]{1,0:T(2,128)}) custom-call(f32[128,2048]{1,0:T(8,128)} %pair_in.1, bf16[128,2048]{1,0:T(8,128)(2,1)} %grad_in.1, bf16[256,1024]{1,0:T(8,128)(2,1)} %bitcast.8, bf16[256,1024]{1,0:T(8,128)(2,1)} %bitcast.9, ...), custom_call_target="tpu_custom_call" | custom-call | tf_op jit(solution)/shard_map/pallas_call | solution.py:716
  117.4 3.1 %shard_map.93 = (f32[128,2048]{1,0:T(8,128)}, bf16[128,2048]{1,0:T(8,128)(2,1)}, f32[256,1024]{1,0:T(8,128)}, f32[256,1024]{1,0:T(8,128)}, f32[2,1024]{1,0:T(2,128)}) custom-call(f32[128,2048]{1,0:T(8,128)} %get-tuple-element.15.refs_0_, bf16[128,2048]{1,0:T(8,128)(2,1)} %get-tuple-element.16.refs_1_, f32[256,1024]{1,0:T(8,128)} %get-tuple-element.17.refs_2_, ...), custom_call_target="tpu_custom_call" | custom-call | tf_op jit(solution)/shard_map/pallas_call | solution.py:786

commit v5 on v4

--- a/solution.py
+++ b/solution.py
@@ -46,6 +46,15 @@
             (f_out, f_put), (g_out, g_put), (in_pair_ref, in_pair_out), (in_grad_ref, in_grad_out),
         ))
     ]
+    split = via.shape[1]
+    results = [
+        pltpu.make_async_copy(result_rx.at[a, :, cols], target.at[:, cols], o_sem.at[slot])
+        for a, target, cols, slot in (
+            (0, f_put, pl.ds(0, split), 0),
+            (1, g_put, pl.ds(0, g_put.shape[1]), 1),
+            (0, f_put, pl.ds(split, f_put.shape[1] - split), 4),
+        )
+    ]
     m = n // 2
     half = sections // 2
     tokens = pair_ref.shape[0]
@@ -572,7 +581,7 @@
             else:
                 direct()
         for a in order:
-            outs[a][...] = product(a, 1 - parity, every)
+            outs[a][...] = product(a, 1 - parity, every).astype(bf16)
             puts[a].start()
 
         @pl.when(routes)
@@ -610,9 +619,7 @@
         puts[3].start()
         for a, cols, slot in (ways[0], ways[2], ways[1]):
             wait_bytes(result_rx.at[a, :, cols], e_recv.at[slot])
-            outs[a][:, cols] = result_rx[a, :, cols].astype(f32)
-            if slot != 1:
-                puts[a].start()
+            results[(0, 2, 1)[slot]].start()
 
     @pl.when(is_mate)
     def _():
@@ -672,33 +679,46 @@
     def _():
         wait_bytes(tx.at[:, pl.ds(0, tokens)], feed_send)
 
-    for put in puts:
+    for put in puts[2:]:
         put.wait()
 
+    @pl.when(is_host)
+    def _():
+        for put in puts[:2]:
+            put.wait()
+
+    @pl.when(is_mate)
+    def _():
+        for result in results:
+            result.wait()
+
 
 def put(k, *refs):
-    sources, targets, held = refs[:k], refs[k:2 * k], refs[2 * k:3 * k]
-    in_sem, out_sem = refs[3 * k:]
-    halves = []
+    sources, targets, held, wide = refs[:k], refs[k:2 * k], refs[2 * k:3 * k], refs[3 * k]
+    in_sem, out_sem = refs[3 * k + 1:]
+    steps, widened = [], 0
     for i in range(k):
         rows = sources[i].shape[0]
         pieces = 2 if rows % 32 == 0 else 1
+        grows = sources[i].dtype != targets[i].dtype
         for c in range(pieces):
             lines = pl.ds(c * (rows // pieces), rows // pieces)
-            halves.append((
-                pltpu.make_async_copy(
-                    sources[i].at[lines], held[i].at[lines], in_sem.at[i, c]
-                ),
-                pltpu.make_async_copy(
-                    held[i].at[lines], targets[i].at[lines], out_sem.at[i, c]
-                ),
-            ))
-    for taken, _ in halves:
+            taken = pltpu.make_async_copy(
+                sources[i].at[lines], held[i].at[lines], in_sem.at[i, c]
+            )
+            source = wide.at[widened, lines] if grows else held[i].at[lines]
+            given = pltpu.make_async_copy(source, targets[i].at[lines], out_sem.at[i, c])
+            steps.append((taken, given, (i, widened, lines) if grows else None))
+        widened += int(grows)
+    for taken, _, _ in steps:
         taken.start()
-    for taken, given in halves:
+    for taken, given, grow in steps:
         taken.wait()
+        if grow is not None:
+            i, place, lines = grow
+            wide[place, lines] = held[i][lines].astype(f32)
         given.start()
-    for _, given in halves:
+    for _, given, _ in steps:
         given.wait()
 
 
@@ -718,8 +738,8 @@
         out_shape=(
             jax.ShapeDtypeStruct((tokens, width), f32),
             jax.ShapeDtypeStruct((tokens, width), bf16),
-            jax.ShapeDtypeStruct((part, h), f32),
-            jax.ShapeDtypeStruct((part, h), f32),
+            jax.ShapeDtypeStruct((part, h), bf16),
+            jax.ShapeDtypeStruct((part, h), bf16),
             jax.ShapeDtypeStruct((2, h), f32),
         ),
         in_specs=[anywhere] * 5,
@@ -732,8 +752,8 @@
             pltpu.VMEM((2, h), f32),
             pltpu.VMEM((tokens, width), f32),
             pltpu.VMEM((tokens, width), bf16),
-            pltpu.VMEM((part, h), f32),
-            pltpu.VMEM((part, h), f32),
+            pltpu.VMEM((part, h), bf16),
+            pltpu.VMEM((part, h), bf16),
             pltpu.VMEM((h, h), bf16),
             pltpu.VMEM((h, h), bf16),
             pltpu.VMEM((h, h), bf16),
@@ -777,7 +797,7 @@
             dma,
             dma((blocks,)),
             dma((5,)),
-            dma((4,)),
+            dma((5,)),
         ],
         compiler_params=pltpu.CompilerParams(
             collective_id=0, has_side_effects=True, vmem_limit_bytes=60 * 1024 * 1024
@@ -785,11 +805,14 @@
     )(out_pair, out_grad, f_weight[0], g_weight[0], gains[0])
     outs = pl.pallas_call(
         functools.partial(put, len(outs)),
-        out_shape=tuple(jax.ShapeDtypeStruct(out.shape, out.dtype) for out in outs),
+        out_shape=tuple(
+            jax.ShapeDtypeStruct(out.shape, bf16 if i == 1 else f32) for i, out in enumerate(outs)
+        ),
         in_specs=[anywhere] * len(outs),
         out_specs=[anywhere] * len(outs),
         scratch_shapes=[
             *(pltpu.VMEM(out.shape, out.dtype) for out in outs),
+            pltpu.VMEM((2, part, h), f32),
             dma((len(outs), 2)),
             dma((len(outs), 2)),
         ],

time: 121 us -> 120 us (level)
  no operation moved by 1% of the time
where the time goes in v5:
time: 120 us
  Pallas kernels  119 us (99%)
    pallas_call x1, Pallas kernels, shards(): pl.pallas_call(functools.partial(kernel, n, sections, blocks), out_shape=...  116 us
    pallas_call x1, Pallas kernels, shards(): pl.pallas_call(functools.partial(put, len(outs)), out_shape=tuple((jax.Sh...  3.05 us

profile of v5, /device:TPU:0, one launch (start us, length us, event | category | flops | bytes accessed | tf_op | source)
XLA Modules:
  0.0 120.1 jit_solution(16860382944873233905)
XLA Ops:
  0.6 116.4 %shard_map.92 = (f32[128,2048]{1,0:T(8,128)}, bf16[128,2048]{1,0:T(8,128)(2,1)}, bf16[256,1024]{1,0:T(8,128)(2,1)}, bf16[256,1024]{1,0:T(8,128)(2,1)}, f32[2,1024]{1,0:T(2,128)}) custom-call(f32[128,2048]{1,0:T(8,128)} %pair_in.1, bf16[128,2048]{1,0:T(8,128)(2,1)} %grad_in.1, bf16[256,1024]{1,0:T(8,128)(2,1)} %bitcast.8, bf16[256,1024]{1,0:T(8,128)(2,1)} %bitcast.9, ...), custom_call_target="tpu_custom_call" | custom-call | tf_op jit(solution)/shard_map/pallas_call | solution.py:736
  117.0 3.0 %shard_map.93 = (f32[128,2048]{1,0:T(8,128)}, bf16[128,2048]{1,0:T(8,128)(2,1)}, f32[256,1024]{1,0:T(8,128)}, f32[256,1024]{1,0:T(8,128)}, f32[2,1024]{1,0:T(2,128)}) custom-call(f32[128,2048]{1,0:T(8,128)} %get-tuple-element.15.refs_0_, bf16[128,2048]{1,0:T(8,128)(2,1)} %get-tuple-element.16.refs_1_, bf16[256,1024]{1,0:T(8,128)(2,1)} %get-tuple-element.17.refs_2_, ...), custom_call_target="tpu_custom_call" | custom-call | tf_op jit(solution)/shard_map/pallas_call | solution.py:806

commit v6 on v5

--- a/solution.py
+++ b/solution.py
@@ -580,13 +580,13 @@
                         )
             else:
                 direct()
+        @pl.when(routes)
+        def _():
+            lax.fori_loop(0, blocks, forward, 0)
+
         for a in order:
             outs[a][...] = product(a, 1 - parity, every).astype(bf16)
             puts[a].start()
-
-        @pl.when(routes)
-        def _():
-            lax.fori_loop(0, blocks, forward, 0)
 
         @pl.when(high)
         def _():

time: 120 us -> 120 us (level)
  no operation moved by 1% of the time
where the time goes in v6:
time: 120 us
  Pallas kernels  119 us (99%)
    pallas_call x1, Pallas kernels, shards(): pl.pallas_call(functools.partial(kernel, n, sections, blocks), out_shape=...  116 us
    pallas_call x1, Pallas kernels, shards(): pl.pallas_call(functools.partial(put, len(outs)), out_shape=tuple((jax.Sh...  3.05 us

profile of v6, /device:TPU:0, one launch (start us, length us, event | category | flops | bytes accessed | tf_op | source)
XLA Modules:
  0.0 120.1 jit_solution(8557295039503151015)
XLA Ops:
  0.6 116.4 %shard_map.92 = (f32[128,2048]{1,0:T(8,128)}, bf16[128,2048]{1,0:T(8,128)(2,1)}, bf16[256,1024]{1,0:T(8,128)(2,1)}, bf16[256,1024]{1,0:T(8,128)(2,1)}, f32[2,1024]{1,0:T(2,128)}) custom-call(f32[128,2048]{1,0:T(8,128)} %pair_in.1, bf16[128,2048]{1,0:T(8,128)(2,1)} %grad_in.1, bf16[256,1024]{1,0:T(8,128)(2,1)} %bitcast.8, bf16[256,1024]{1,0:T(8,128)(2,1)} %bitcast.9, ...), custom_call_target="tpu_custom_call" | custom-call | tf_op jit(solution)/shard_map/pallas_call | solution.py:736
  117.0 3.0 %shard_map.93 = (f32[128,2048]{1,0:T(8,128)}, bf16[128,2048]{1,0:T(8,128)(2,1)}, f32[256,1024]{1,0:T(8,128)}, f32[256,1024]{1,0:T(8,128)}, f32[2,1024]{1,0:T(2,128)}) custom-call(f32[128,2048]{1,0:T(8,128)} %get-tuple-element.15.refs_0_, bf16[128,2048]{1,0:T(8,128)(2,1)} %get-tuple-element.16.refs_1_, bf16[256,1024]{1,0:T(8,128)(2,1)} %get-tuple-element.17.refs_2_, ...), custom_call_target="tpu_custom_call" | custom-call | tf_op jit(solution)/shard_map/pallas_call | solution.py:806
